TPU v7x, 256 devices: a whole 4x4x8 slice. The times are simulated.
256 devices in a mesh: gx: 8 (over z), gy: 8 (over y, x_hi), gz: 4 (over x_lo, core).
Axes of the slice: x: 4 (x_hi: 2, x_lo: 2; x = x_hi * 2 + x_lo), y: 4, z: 8, core: 2. Of those that a mesh axis runs over, the one named last changes fastest.
Arguments:
- hidden_acts: bfloat16 [4, 8, 8, 256, 16384], P('gz', 'gy', 'gx'), may hold values from -6 to 6
- output_grad: bfloat16 [4, 8, 8, 256, 32], P('gz', 'gy', 'gx'), may hold values from -6 to 6
- weights: bfloat16 [4, 8, 8, 32, 16384], P('gz', 'gy', 'gx'), may hold values from -6 to 6
- momentum: bfloat16 [4, 8, 8, 32, 16384], P('gz', 'gy', 'gx'), may hold values from -48 to 48
- worker_of_slot: int32 [256], replicated, may hold values from 0 to 255, each once
- round_shift: int32 [8], replicated, may hold values from 0 to 7, as said below
Outputs:
- mixed: bfloat16 [8, 8, 4, 32, 16384], P('gx', 'gy', 'gz')
- new_momentum: bfloat16 [4, 8, 8, 32, 16384], P('gz', 'gy', 'gx')
Inputs may be any that keep to these rules, and one draw needn't show every extreme that they name: `round_shift`: each entry is below log2 of 256, so offsets are powers of two below 256; some round has offset 256 / 2 and some round offset 1.
All inputs are finite; a program needn't handle non-finite values.
Results may differ from a plain program's by a relative error of at most 0.0081.
Values may be sent and summed in bfloat16 or wider, within the bound.
A program may use at most 64 MiB of HBM per device.

v0:
```python
import jax
import jax.numpy as jnp
from jax import lax
from jax.sharding import PartitionSpec as P

ROUNDS = 8


learn_rate = 0.01
beta_keep = 0.9


def in_blocks(shard, dim, count):
    lengths = shard.shape
    tiles = shard.reshape(*lengths[:dim], count, lengths[dim] // count, *lengths[dim + 1 :])
    return jnp.moveaxis(tiles, dim, 0)


def joined_along(tiles, dim):
    lengths = list(tiles.shape[1:])
    lengths[dim] *= tiles.shape[0]
    return jnp.moveaxis(tiles, 0, dim).reshape(lengths)


def exchange_both(shard, axis, axes, splits, concats):
    sizes = [lax.axis_size(a) for a in axes]
    tiles = in_blocks(shard, splits[0], sizes[0])
    tiles = jnp.moveaxis(in_blocks(tiles, splits[1] + 1, sizes[1]), 0, 1)
    inside = tiles.shape[2:]
    tiles = tiles.reshape(-1, *inside)
    tiles = lax.all_to_all(tiles, axis, split_axis=0, concat_axis=0, tiled=True)
    tiles = joined_along(tiles.reshape(*sizes, *inside), concats[0] + 1)
    return joined_along(tiles, concats[1])


def for_sending(shard):
    return jax.tree.map(lambda a: a.astype(jnp.bfloat16) if a.dtype == jnp.float32 else a, shard)


def shifted(value, axis, steps):
    count = lax.axis_size(axis)
    pairs = [(source, (source + steps) % count) for source in range(count)]
    return lax.ppermute(value, axis, pairs)


def spread(block, select, outer, workers):
    pieces = block.reshape(outer, workers // outer, block.size // workers)
    moved = exchange_both(pieces, ("gx", "gy", "gz"), ("gx", ("gy", "gz")), (0, 1), (0, 1))
    rows_all = jnp.take(moved.reshape(workers, -1), select, axis=0)
    back = lax.all_to_all(
        lax.all_to_all(
            rows_all.reshape(pieces.shape), "gx", split_axis=0, concat_axis=0, tiled=True
        ),
        ("gy", "gz"),
        split_axis=1,
        concat_axis=1,
        tiled=True,
    )
    return back.reshape(block.shape)


def from_all(value, power):
    return jax.tree.map(
        lambda part, own: part.astype(own.dtype),
        shifted(for_sending(value), ("gx", "gy", "gz"), 1 << power),
        value,
    )


def shards(hidden_acts, output_grad, weights, momentum, worker_of_slot, round_shift):
    hidden = hidden_acts.reshape(hidden_acts.shape[-2:])
    grad_out = output_grad.reshape(output_grad.shape[-2:])
    weight = weights.reshape(weights.shape[-2:])
    moment = momentum.reshape(momentum.shape[-2:])
    grad = lax.dot_general(
        grad_out, hidden, (((0,), (0,)), ((), ())), preferred_element_type=jnp.float32
    )
    velocity = beta_keep * moment.astype(jnp.float32) + grad
    new_moment = velocity.astype(jnp.bfloat16)
    stepped = (weight.astype(jnp.float32) - learn_rate * velocity).astype(jnp.bfloat16)
    count_x = lax.axis_size("gx")
    count_y = lax.axis_size("gy")
    count_z = lax.axis_size("gz")
    workers = count_x * count_y * count_z
    joined = jnp.arange(workers, dtype=jnp.int32)
    digit_x = joined // (count_y * count_z)
    digit_y = joined // count_z % count_y
    digit_z = joined % count_z
    slots = digit_x + count_x * (digit_y + count_y * digit_z)
    held = jnp.take(worker_of_slot, slots, axis=0)
    source = jnp.zeros((workers,), jnp.int32).at[held].set(joined)
    levels = workers.bit_length() - 1
    branches = []
    block = spread(stepped, source, count_x, workers)
    for level in range(levels):
        branches.append(lambda value, power=level: from_all(value, power))
    for step in range(ROUNDS):
        received = lax.switch(round_shift[step], branches, block)
        block = ((block.astype(jnp.float32) + received.astype(jnp.float32)) * 0.5).astype(
            jnp.bfloat16
        )
    return (block.reshape(weights.shape), new_moment.reshape(momentum.shape))


def solution(mesh):
    placed = (
        P("gz", "gy", "gx", None, None),
        P("gz", "gy", "gx", None, None),
        P("gz", "gy", "gx", None, None),
        P("gz", "gy", "gx", None, None),
        P(),
        P(),
    )
    return jax.shard_map(
        shards,
        mesh=mesh,
        in_specs=placed,
        out_specs=(P("gx", "gy", "gz", None, None), P("gz", "gy", "gx", None, None)),
        check_vma=False,
    )
```

profile of v0, /device:TPU:0, one launch (start us, length us, event | category | flops | bytes accessed | tf_op | source)
XLA Modules:
  0.0 417.5 jit_solution(10497113891742632701)
XLA Ops:
  0.6 0.0 copy-start
  0.6 0.7 copy-done
  1.4 6.6 %convert_bitcast_fusion = (bf16[1,1,1,32,16384]{4,3,2,1,0:T(8,128)(2,1)}, bf16[32,16384]{1,0:T(8,128)(2,1)S(1)}) fusion(bf16[1,1,1,32,16384]{4,3,2,1,0:T(8,128)(2,1)} %param.72, bf16[1,1,1,256,16384]{4,3,2,1,0:T(8,128)(2,1)} %param.70, bf16[1,1,1,256,32]{3,4,2,1,0:T(8,128)(2,1)S(1)} %copy-done, bf16[1,1,1,32,16384]{4,3,2,1,0:T(8,128)(2,1)} %param.73), kind=kOutput, calls=%fused_computation.17 | convolution fusion | flops 272629760 | bytes 12599296 | tf_op jit(solution)/shard_map/dot_general | solution.py:75
  7.9 1.6 reshape_transpose_transpose_reshape_reshape_reshape.4
  9.6 0.5 broadcast.402
  10.1 6.8 %reduce = bf16[256,2048]{1,0:T(8,128)(2,1)S(1)} reduce(bf16[256,1,1,2048]{3,2,1,0:T(2,128)(2,1)S(1)} %reshape_transpose_transpose_reshape_reshape_reshape.4, bf16[]{:T(256)} %broadcast.402), dimensions={1,2}, to_apply=%reshape_transpose_transpose_reshape_reshape_reshape.4.reduce_sub_computation | reduce | bytes 2097154 | tf_op jit(solution)/shard_map/reshape;transpose;transpose;reshape;reshape;reshape | solution.py:30
  16.9 0.0 copy-start.1
  16.9 1.6 reshape.285
  18.5 15.7 %all-to-all-start = ((bf16[256,2,1024]{2,1,0:T(2,128)(2,1)}), bf16[256,2,1024]{2,1,0:T(2,128)(2,1)}, u32[]{:S(2)}, u32[]{:S(2)}) async-start(bf16[256,2,1024]{2,1,0:T(2,128)(2,1)} %reshape.285), calls=%async_computation | async-start | bytes 2097152 | tf_op jit(solution)/shard_map/all_to_all | solution.py:31
  34.2 0.0 copy-done.1
  34.2 1.9 gather_fusion
  36.2 1.7 scatter_custom_fusion
  37.8 0.1 broadcast_in_dim.22
  37.9 25.0 %all-to-all-done = bf16[256,2,1024]{2,1,0:T(2,128)(2,1)} async-done(((bf16[256,2,1024]{2,1,0:T(2,128)(2,1)}), bf16[256,2,1024]{2,1,0:T(2,128)(2,1)}, u32[]{:S(2)}, u32[]{:S(2)}) %all-to-all-start) | async-done | bytes 1048608 | tf_op jit(solution)/shard_map/all_to_all | solution.py:31
  62.9 6.4 %reshape.286 = bf16[256,1,1,2048]{3,2,1,0:T(2,128)(2,1)S(1)} reshape(bf16[256,2,1024]{2,1,0:T(2,128)(2,1)} %all-to-all-done) | data formatting | bytes 2097152
  69.3 0.6 copy.19
  69.9 1.4 gather_fusion.1
  71.3 0.2 broadcast_select_fusion
  71.5 32.1 %all_to_all.15 = bf16[8,32,2048]{2,1,0:T(8,128)(2,1)S(1)} all-to-all(bf16[8,32,2048]{2,1,0:T(8,128)(2,1)S(1)} %broadcast_select_fusion), channel_id=1, replica_groups=mesh['gx'=8,'gy'=8,'gz'=4] {'gx'}, dimensions={0} | all-to-all | bytes 2097152 | tf_op jit(solution)/shard_map/all_to_all | solution.py:51
  103.5 0.0 copy-start.2
  103.5 1.5 copy.15
  105.1 4.2 %all-to-all-start.2 = ((bf16[8,32,2048]{2,0,1:T(8,128)(2,1)}), bf16[8,32,2048]{2,0,1:T(8,128)(2,1)S(1)}, u32[]{:S(2)}, u32[]{:S(2)}) async-start(bf16[8,32,2048]{2,0,1:T(8,128)(2,1)} %copy.15), calls=%async_computation.2 | async-start | bytes 2097152 | tf_op jit(solution)/shard_map/all_to_all | solution.py:50
  109.3 0.0 copy-done.2
  109.3 0.7 fusion.11
  115.1 11.4 %all-to-all-done.2 = bf16[8,32,2048]{2,0,1:T(8,128)(2,1)S(1)} async-done(((bf16[8,32,2048]{2,0,1:T(8,128)(2,1)}), bf16[8,32,2048]{2,0,1:T(8,128)(2,1)S(1)}, u32[]{:S(2)}, u32[]{:S(2)}) %all-to-all-start.2) | async-done | bytes 1048608 | tf_op jit(solution)/shard_map/all_to_all | solution.py:50
  126.5 0.6 copy.16
  127.1 0.5 reshape.254
  127.6 31.1 %conditional.32 = (bf16[32,16384]{1,0:T(8,128)(2,1)}) conditional(s32[]{:T(128)} %bitcast.12, bf16[32,16384]{1,0:T(8,128)(2,1)S(1)} %reshape.254, bf16[32,16384]{1,0:T(8,128)(2,1)S(1)} %reshape.254, bf16[32,16384]{1,0:T(8,128)(2,1)S(1)} %reshape.254, bf16[32,16384]{1,0:T(8,128)(2,1)S(1)} %reshape.254, ...), branch_computations={%region_1.2_spmd, %region_2.3_spmd, %region_3.4_spmd, %region_4.5_... | conditional | bytes 4194352
  127.6 1.4 collective-permute-start.2
  129.1 29.7 %collective-permute-done.2 = bf16[32,16384]{1,0:T(8,128)(2,1)} collective-permute-done((bf16[32,16384]{1,0:T(8,128)(2,1)S(1)}, bf16[32,16384]{1,0:T(8,128)(2,1)}, u32[]{:S(2)}, u32[]{:S(2)}) %collective-permute-start.2) | collective-permute-done | bytes 1048608 | tf_op jit(solution)/shard_map/cond/branch_2_fun/ppermute | solution.py:43
  158.7 1.5 multiply_convert_fusion.7
  160.3 58.8 %conditional.33 = (bf16[32,16384]{1,0:T(8,128)(2,1)}) conditional(s32[]{:T(128)} %bitcast.13, bf16[32,16384]{1,0:T(8,128)(2,1)S(1)} %multiply_convert_fusion.7, bf16[32,16384]{1,0:T(8,128)(2,1)S(1)} %multiply_convert_fusion.7, bf16[32,16384]{1,0:T(8,128)(2,1)S(1)} %multiply_convert_fusion.7, ...), branch_computations={%region_9.10_spmd, %region_10.11_spmd, %region_11.12_spmd, %region... | conditional | bytes 4194352
  169.2 0.7 collective-permute-start.15
  169.8 49.2 %collective-permute-done.15 = bf16[32,16384]{1,0:T(8,128)(2,1)} collective-permute-done((bf16[32,16384]{1,0:T(8,128)(2,1)S(1)}, bf16[32,16384]{1,0:T(8,128)(2,1)}, u32[]{:S(2)}, u32[]{:S(2)}) %collective-permute-start.15) | collective-permute-done | bytes 1048608 | tf_op jit(solution)/shard_map/cond/branch_7_fun/ppermute | solution.py:43
  219.0 1.5 multiply_convert_fusion.6
  220.6 47.7 %conditional.34 = (bf16[32,16384]{1,0:T(8,128)(2,1)}) conditional(s32[]{:T(128)} %bitcast.14, bf16[32,16384]{1,0:T(8,128)(2,1)S(1)} %multiply_convert_fusion.6, bf16[32,16384]{1,0:T(8,128)(2,1)S(1)} %multiply_convert_fusion.6, bf16[32,16384]{1,0:T(8,128)(2,1)S(1)} %multiply_convert_fusion.6, ...), branch_computations={%region_17.18_spmd, %region_18.19_spmd, %region_19.20_spmd, %regio... | conditional | bytes 4194352
  220.6 0.1 collective-permute-start.22
  220.7 47.6 %collective-permute-done.22 = bf16[32,16384]{1,0:T(8,128)(2,1)} collective-permute-done((bf16[32,16384]{1,0:T(8,128)(2,1)S(1)}, bf16[32,16384]{1,0:T(8,128)(2,1)}, u32[]{:S(2)}, u32[]{:S(2)}) %collective-permute-start.22) | collective-permute-done | bytes 1048608 | tf_op jit(solution)/shard_map/cond/branch_6_fun/ppermute | solution.py:43
  268.3 1.5 multiply_convert_fusion.5
  269.8 22.6 %conditional.35 = (bf16[32,16384]{1,0:T(8,128)(2,1)}) conditional(s32[]{:T(128)} %bitcast.15, bf16[32,16384]{1,0:T(8,128)(2,1)S(1)} %multiply_convert_fusion.5, bf16[32,16384]{1,0:T(8,128)(2,1)S(1)} %multiply_convert_fusion.5, bf16[32,16384]{1,0:T(8,128)(2,1)S(1)} %multiply_convert_fusion.5, ...), branch_computations={%region_25.26_spmd, %region_26.27_spmd, %region_27.28_spmd, %regio... | conditional | bytes 4194352
  269.8 1.1 collective-permute-start.25
  270.9 21.0 %collective-permute-done.25 = bf16[32,16384]{1,0:T(8,128)(2,1)} collective-permute-done((bf16[32,16384]{1,0:T(8,128)(2,1)S(1)}, bf16[32,16384]{1,0:T(8,128)(2,1)}, u32[]{:S(2)}, u32[]{:S(2)}) %collective-permute-start.25) | collective-permute-done | bytes 1048608 | tf_op jit(solution)/shard_map/cond/branch_1_fun/ppermute | solution.py:43
  292.4 1.5 multiply_convert_fusion.4
  293.9 47.5 %conditional.36 = (bf16[32,16384]{1,0:T(8,128)(2,1)}) conditional(s32[]{:T(128)} %bitcast.16, bf16[32,16384]{1,0:T(8,128)(2,1)S(1)} %multiply_convert_fusion.4, bf16[32,16384]{1,0:T(8,128)(2,1)S(1)} %multiply_convert_fusion.4, bf16[32,16384]{1,0:T(8,128)(2,1)S(1)} %multiply_convert_fusion.4, ...), branch_computations={%region_33.34_spmd, %region_34.35_spmd, %region_35.36_spmd, %regio... | conditional | bytes 4194352
  293.9 0.1 collective-permute-start.39
  294.0 47.4 %collective-permute-done.39 = bf16[32,16384]{1,0:T(8,128)(2,1)} collective-permute-done((bf16[32,16384]{1,0:T(8,128)(2,1)S(1)}, bf16[32,16384]{1,0:T(8,128)(2,1)}, u32[]{:S(2)}, u32[]{:S(2)}) %collective-permute-start.39) | collective-permute-done | bytes 1048608 | tf_op jit(solution)/shard_map/cond/branch_7_fun/ppermute | solution.py:43
  341.5 1.5 multiply_convert_fusion.3
  343.0 28.8 %conditional.37 = (bf16[32,16384]{1,0:T(8,128)(2,1)}) conditional(s32[]{:T(128)} %bitcast.17, bf16[32,16384]{1,0:T(8,128)(2,1)S(1)} %multiply_convert_fusion.3, bf16[32,16384]{1,0:T(8,128)(2,1)S(1)} %multiply_convert_fusion.3, bf16[32,16384]{1,0:T(8,128)(2,1)S(1)} %multiply_convert_fusion.3, ...), branch_computations={%region_41.42_spmd, %region_42.43_spmd, %region_43.44_spmd, %regio... | conditional | bytes 4194352
  343.0 3.0 collective-permute-start.42
  346.0 25.6 %collective-permute-done.42 = bf16[32,16384]{1,0:T(8,128)(2,1)} collective-permute-done((bf16[32,16384]{1,0:T(8,128)(2,1)S(1)}, bf16[32,16384]{1,0:T(8,128)(2,1)}, u32[]{:S(2)}, u32[]{:S(2)}) %collective-permute-start.42) | collective-permute-done | bytes 1048608 | tf_op jit(solution)/shard_map/cond/branch_2_fun/ppermute | solution.py:43
  371.8 1.5 multiply_convert_fusion.2
  373.3 19.9 %conditional.38 = (bf16[32,16384]{1,0:T(8,128)(2,1)}) conditional(s32[]{:T(128)} %bitcast.18, bf16[32,16384]{1,0:T(8,128)(2,1)S(1)} %multiply_convert_fusion.2, bf16[32,16384]{1,0:T(8,128)(2,1)S(1)} %multiply_convert_fusion.2, bf16[32,16384]{1,0:T(8,128)(2,1)S(1)} %multiply_convert_fusion.2, ...), branch_computations={%region_49.50_spmd, %region_50.51_spmd, %region_51.52_spmd, %regio... | conditional | bytes 4194352
  373.3 0.1 collective-permute-start.48
  373.4 19.7 %collective-permute-done.48 = bf16[32,16384]{1,0:T(8,128)(2,1)} collective-permute-done((bf16[32,16384]{1,0:T(8,128)(2,1)S(1)}, bf16[32,16384]{1,0:T(8,128)(2,1)}, u32[]{:S(2)}, u32[]{:S(2)}) %collective-permute-start.48) | collective-permute-done | bytes 1048608 | tf_op jit(solution)/shard_map/cond/branch_0_fun/ppermute | solution.py:43
  393.1 1.5 multiply_convert_fusion.1
  394.7 20.0 %conditional.39 = (bf16[32,16384]{1,0:T(8,128)(2,1)}) conditional(s32[]{:T(128)} %bitcast.19, bf16[32,16384]{1,0:T(8,128)(2,1)S(1)} %multiply_convert_fusion.1, bf16[32,16384]{1,0:T(8,128)(2,1)S(1)} %multiply_convert_fusion.1, bf16[32,16384]{1,0:T(8,128)(2,1)S(1)} %multiply_convert_fusion.1, ...), branch_computations={%region_57.58_spmd, %region_58.59_spmd, %region_59.60_spmd, %regio... | conditional | bytes 4194352
  394.7 0.1 collective-permute-start.56
  394.8 19.7 %collective-permute-done.56 = bf16[32,16384]{1,0:T(8,128)(2,1)} collective-permute-done((bf16[32,16384]{1,0:T(8,128)(2,1)S(1)}, bf16[32,16384]{1,0:T(8,128)(2,1)}, u32[]{:S(2)}, u32[]{:S(2)}) %collective-permute-start.56) | collective-permute-done | bytes 1048608 | tf_op jit(solution)/shard_map/cond/branch_0_fun/ppermute | solution.py:43
  414.7 2.5 fusion.2
  (7 shorter events, 0.1 us)
Async XLA Ops:
  0.6 0.7 copy-start
  16.9 17.3 %copy-start.1 = (s32[256]{0:T(256)S(1)}, s32[256]{0:T(256)}, u32[]{:S(2)}) copy-start(s32[256]{0:T(256)} %param.74) | copy-start | bytes 3076
  18.5 44.5 %all-to-all-start = ((bf16[256,2,1024]{2,1,0:T(2,128)(2,1)}), bf16[256,2,1024]{2,1,0:T(2,128)(2,1)}, u32[]{:S(2)}, u32[]{:S(2)}) async-start(bf16[256,2,1024]{2,1,0:T(2,128)(2,1)} %reshape.285), calls=%async_computation | async-start | bytes 2097152 | tf_op jit(solution)/shard_map/all_to_all | solution.py:31
  103.5 5.7 %copy-start.2 = (s32[8]{0:T(128)S(1)}, s32[8]{0:T(128)}, u32[]{:S(2)}) copy-start(s32[8]{0:T(128)} %param.75) | copy-start | bytes 100
  105.1 21.4 %all-to-all-start.2 = ((bf16[8,32,2048]{2,0,1:T(8,128)(2,1)}), bf16[8,32,2048]{2,0,1:T(8,128)(2,1)S(1)}, u32[]{:S(2)}, u32[]{:S(2)}) async-start(bf16[8,32,2048]{2,0,1:T(8,128)(2,1)} %copy.15), calls=%async_computation.2 | async-start | bytes 2097152 | tf_op jit(solution)/shard_map/all_to_all | solution.py:50
  127.6 31.1 %collective-permute-start.2 = (bf16[32,16384]{1,0:T(8,128)(2,1)S(1)}, bf16[32,16384]{1,0:T(8,128)(2,1)}, u32[]{:S(2)}, u32[]{:S(2)}) collective-permute-start(bf16[32,16384]{1,0:T(8,128)(2,1)S(1)} %param.2), channel_id=1, source_target_pairs={{0,4},{1,5},{2,6},{3,7},{4,8},{5,9},{6,10},{7,11},{8,12},{9,13},{1... | collective-permute-start | bytes 3145736 | tf_op jit(solution)/shard_map/cond/branch_2_fun/ppermute | solution.py:43
  169.2 49.8 %collective-permute-start.15 = (bf16[32,16384]{1,0:T(8,128)(2,1)S(1)}, bf16[32,16384]{1,0:T(8,128)(2,1)}, u32[]{:S(2)}, u32[]{:S(2)}) collective-permute-start(bf16[32,16384]{1,0:T(8,128)(2,1)S(1)} %param.15), channel_id=1, source_target_pairs={{0,128},{1,129},{2,130},{3,131},{4,132},{5,133},{6,134},{7,135},{8... | collective-permute-start | bytes 3145736 | tf_op jit(solution)/shard_map/cond/branch_7_fun/ppermute | solution.py:43
  220.6 47.7 %collective-permute-start.22 = (bf16[32,16384]{1,0:T(8,128)(2,1)S(1)}, bf16[32,16384]{1,0:T(8,128)(2,1)}, u32[]{:S(2)}, u32[]{:S(2)}) collective-permute-start(bf16[32,16384]{1,0:T(8,128)(2,1)S(1)} %param.22), channel_id=1, source_target_pairs={{0,64},{1,65},{2,66},{3,67},{4,68},{5,69},{6,70},{7,71},{8,72},{9,... | collective-permute-start | bytes 3145736 | tf_op jit(solution)/shard_map/cond/branch_6_fun/ppermute | solution.py:43
  269.8 22.2 %collective-permute-start.25 = (bf16[32,16384]{1,0:T(8,128)(2,1)S(1)}, bf16[32,16384]{1,0:T(8,128)(2,1)}, u32[]{:S(2)}, u32[]{:S(2)}) collective-permute-start(bf16[32,16384]{1,0:T(8,128)(2,1)S(1)} %param.25), channel_id=1, source_target_pairs={{0,2},{1,3},{2,4},{3,5},{4,6},{5,7},{6,8},{7,9},{8,10},{9,11},{10,... | collective-permute-start | bytes 3145736 | tf_op jit(solution)/shard_map/cond/branch_1_fun/ppermute | solution.py:43
  293.9 47.5 %collective-permute-start.39 = (bf16[32,16384]{1,0:T(8,128)(2,1)S(1)}, bf16[32,16384]{1,0:T(8,128)(2,1)}, u32[]{:S(2)}, u32[]{:S(2)}) collective-permute-start(bf16[32,16384]{1,0:T(8,128)(2,1)S(1)} %param.39), channel_id=1, source_target_pairs={{0,128},{1,129},{2,130},{3,131},{4,132},{5,133},{6,134},{7,135},{8... | collective-permute-start | bytes 3145736 | tf_op jit(solution)/shard_map/cond/branch_7_fun/ppermute | solution.py:43
  343.0 28.6 %collective-permute-start.42 = (bf16[32,16384]{1,0:T(8,128)(2,1)S(1)}, bf16[32,16384]{1,0:T(8,128)(2,1)}, u32[]{:S(2)}, u32[]{:S(2)}) collective-permute-start(bf16[32,16384]{1,0:T(8,128)(2,1)S(1)} %param.42), channel_id=1, source_target_pairs={{0,4},{1,5},{2,6},{3,7},{4,8},{5,9},{6,10},{7,11},{8,12},{9,13},{1... | collective-permute-start | bytes 3145736 | tf_op jit(solution)/shard_map/cond/branch_2_fun/ppermute | solution.py:43
  373.3 19.8 %collective-permute-start.48 = (bf16[32,16384]{1,0:T(8,128)(2,1)S(1)}, bf16[32,16384]{1,0:T(8,128)(2,1)}, u32[]{:S(2)}, u32[]{:S(2)}) collective-permute-start(bf16[32,16384]{1,0:T(8,128)(2,1)S(1)} %param.48), channel_id=1, source_target_pairs={{0,1},{1,2},{2,3},{3,4},{4,5},{5,6},{6,7},{7,8},{8,9},{9,10},{10,1... | collective-permute-start | bytes 3145736 | tf_op jit(solution)/shard_map/cond/branch_0_fun/ppermute | solution.py:43
  394.7 19.8 %collective-permute-start.56 = (bf16[32,16384]{1,0:T(8,128)(2,1)S(1)}, bf16[32,16384]{1,0:T(8,128)(2,1)}, u32[]{:S(2)}, u32[]{:S(2)}) collective-permute-start(bf16[32,16384]{1,0:T(8,128)(2,1)S(1)} %param.56), channel_id=1, source_target_pairs={{0,1},{1,2},{2,3},{3,4},{4,5},{5,6},{6,7},{7,8},{8,9},{9,10},{10,1... | collective-permute-start | bytes 3145736 | tf_op jit(solution)/shard_map/cond/branch_0_fun/ppermute | solution.py:43
where the time goes:
time: 413 us; the launch traced here: 417 us
  waiting for transfers between devices  296 us (72%)
  blocking collectives  32.1 us (8%)
  starting transfers between devices  26.4 us (6%)
  other arithmetic  20.2 us (5%)
  local copies, waits for them, and re-layouts  19.8 us (5%)
  loops' own time  9.85 us (2%)
  matrix products  6.59 us (2%)
  between operations  6.16 us (1%)
    ppermute x8, waiting for transfers between devices, shifted(): return lax.ppermute(value, axis, pairs)  260 us
    all_to_all x1, blocking collectives, spread(): lax.all_to_all(rows_all.reshape(pieces.shape), 'gx', split_axis=0, concat...  32.1 us
    all_to_all x1, waiting for transfers between devices, exchange_both(): tiles = lax.all_to_all(tiles, axis, split_axis=0, concat_axis=0, tiled=True)  25 us
    all_to_all x1, starting transfers between devices, exchange_both(): tiles = lax.all_to_all(tiles, axis, split_axis=0, concat_axis=0, tiled=True)  15.7 us
    all_to_all x1, waiting for transfers between devices, spread(): lax.all_to_all(lax.all_to_all(rows_all.reshape(pieces.shape), 'gx', split...  11.4 us
    convert_element_type x7, other arithmetic, shards(): ((block.astype(jnp.float32) + received.astype(jnp.float32)) * 0.5).astype...  10.7 us
    unnamed x8, loops' own time  9.85 us
    unnamed x9, local copies, waits for them, and re-layouts  9.31 us
  transfers between devices with their start and end apart: 10, of which 10 were waited for; matrix products, arithmetic and copies ran while one was open for 1% of the time, Pallas kernels for 0%

commit v1 on v0

v1 whole, which is shorter than its diff:
```python
import jax
import jax.numpy as jnp
from jax import lax
from jax.sharding import PartitionSpec as P

ROUNDS = 8
learn_rate = 0.01
beta_keep = 0.9
AXES = ("gx", "gy", "gz")


def mixing(held, round_shift, workers):
    offsets = jnp.left_shift(jnp.int32(1), round_shift)
    half = ROUNDS // 2
    bits = (jnp.arange(1 << half)[:, None] >> jnp.arange(half)[None, :]) & 1
    low = jnp.sum(bits * offsets[:half][None, :], axis=1)
    high = jnp.sum(bits * offsets[half:][None, :], axis=1)
    index = jnp.arange(workers, dtype=jnp.int32)
    first = jnp.zeros((workers, workers), jnp.int32)
    second = jnp.zeros((workers, workers), jnp.int32)
    for m in range(1 << half):
        first += ((held[None, :] + low[m] - index[:, None]) & (workers - 1)) == 0
        second += ((index[None, :] + high[m] - index[:, None]) & (workers - 1)) == 0
    first = (first.astype(jnp.float32) / (1 << half)).astype(jnp.bfloat16)
    second = (second.astype(jnp.float32) / (1 << half)).astype(jnp.bfloat16)
    return jnp.dot(second, first, preferred_element_type=jnp.float32).astype(jnp.bfloat16)


def shards(hidden_acts, output_grad, weights, momentum, worker_of_slot, round_shift):
    hidden = hidden_acts.reshape(hidden_acts.shape[-2:])
    grad_out = output_grad.reshape(output_grad.shape[-2:])
    weight = weights.reshape(weights.shape[-2:])
    moment = momentum.reshape(momentum.shape[-2:])
    grad = lax.dot_general(
        grad_out, hidden, (((0,), (0,)), ((), ())), preferred_element_type=jnp.float32
    )
    velocity = beta_keep * moment.astype(jnp.float32) + grad
    new_moment = velocity.astype(jnp.bfloat16)
    stepped = (weight.astype(jnp.float32) - learn_rate * velocity).astype(jnp.bfloat16)
    count_x = lax.axis_size("gx")
    count_y = lax.axis_size("gy")
    count_z = lax.axis_size("gz")
    workers = count_x * count_y * count_z
    held = worker_of_slot.reshape(count_z, count_y, count_x).transpose(2, 1, 0).reshape(-1)
    mix = mixing(held, round_shift, workers)
    pieces = stepped.reshape(workers, -1)
    moved = lax.all_to_all(pieces, AXES, split_axis=0, concat_axis=0, tiled=True)
    mixed = jnp.dot(mix, moved, preferred_element_type=jnp.float32).astype(jnp.bfloat16)
    back = lax.all_to_all(mixed, AXES, split_axis=0, concat_axis=0, tiled=True)
    return (back.reshape(weights.shape), new_moment.reshape(momentum.shape))


def solution(mesh):
    placed = (
        P("gz", "gy", "gx", None, None),
        P("gz", "gy", "gx", None, None),
        P("gz", "gy", "gx", None, None),
        P("gz", "gy", "gx", None, None),
        P(),
        P(),
    )
    return jax.shard_map(
        shards,
        mesh=mesh,
        in_specs=placed,
        out_specs=(P("gx", "gy", "gz", None, None), P("gz", "gy", "gx", None, None)),
        check_vma=False,
    )
```

time: 413 us -> 122 us (0.30)
  the two profiles are of different devices: /device:TPU:0 before, /device:TPU:1 now
where the time goes in v1:
time: 122 us; the launch traced here: 121 us
  blocking collectives  40.4 us (33%)
  other arithmetic  35.5 us (29%)
  starting transfers between devices  15.7 us (13%)
  local copies, waits for them, and re-layouts  15.1 us (12%)
  matrix products  9.96 us (8%)
  waiting for transfers between devices  3.69 us (3%)
    all_to_all x1, blocking collectives, shards(): back = lax.all_to_all(mixed, AXES, split_axis=0, concat_axis=0, tiled=True)  40.4 us
    all_to_all x1, starting transfers between devices, shards(): lax.all_to_all(pieces, AXES, split_axis=0, concat_axis=0, tiled=True)  15.7 us
    add x16, other arithmetic, mixing(): second += index[None, :] + high[m] - index[:, None] & workers - 1 == 0  9.9 us
    add x1, other arithmetic, mixing(): first += held[None, :] + low[m] - index[:, None] & workers - 1 == 0  9.87 us
    all_to_all x2, other arithmetic, shards(): back = lax.all_to_all(mixed, AXES, split_axis=0, concat_axis=0, tiled=True)  8.83 us
    all_to_all x1, other arithmetic, shards(): lax.all_to_all(pieces, AXES, split_axis=0, concat_axis=0, tiled=True)  6.84 us
    dot_general x1, matrix products, shards(): lax.dot_general(grad_out, hidden, (((0,), (0,)), ((), ())), preferred_ele...  6.59 us
    add x48, local copies, waits for them, and re-layouts, mixing(): first += held[None, :] + low[m] - index[:, None] & workers - 1 == 0  5.29 us
  transfers between devices with their start and end apart: 1, of which 1 were waited for; matrix products, arithmetic and copies ran while one was open for 22% of the time, Pallas kernels for 0%

profile of v1, /device:TPU:1, one launch (start us, length us, event | category | flops | bytes accessed | tf_op | source)
XLA Modules:
  0.0 121.3 jit_solution(561392824004067641)
XLA Ops:
  0.6 0.7 copy-done
  1.4 6.6 %convert_bitcast_fusion = (bf16[1,1,1,32,16384]{4,3,2,1,0:T(8,128)(2,1)}, bf16[32,16384]{1,0:T(8,128)(2,1)S(1)}) fusion(bf16[1,1,1,32,16384]{4,3,2,1,0:T(8,128)(2,1)} %param.8, bf16[1,1,1,256,16384]{4,3,2,1,0:T(8,128)(2,1)} %param.6, bf16[1,1,1,256,32]{3,4,2,1,0:T(8,128)(2,1)S(1)} %copy-done, bf16[1,1,1,32,16384]{4,3,2,1,0:T(8,128)(2,1)} %param.9), kind=kOutput, calls=%fused_computation.9 | convolution fusion | flops 272629760 | bytes 12599296 | tf_op jit(solution)/shard_map/dot_general | solution.py:34
  7.9 1.6 %all_to_all.19 = bf16[256,1,2048]{2,1,0:T(2,128)(2,1)S(1)} reshape(bf16[32,16384]{1,0:T(8,128)(2,1)S(1)} %get-tuple-element.3) | data formatting | bytes 2097152 | tf_op jit(solution)/shard_map/all_to_all | solution.py:47
  9.6 0.6 broadcast.301
  10.1 6.8 %reduce.1 = bf16[256,2048]{1,0:T(8,128)(2,1)S(1)} reduce(bf16[256,1,2048]{2,1,0:T(2,128)(2,1)S(1)} %all_to_all.19, bf16[]{:T(256)} %broadcast.301), dimensions={1}, to_apply=%all_to_all.19.reduce_sub_computation | reduce | bytes 2097154 | tf_op jit(solution)/shard_map/all_to_all | solution.py:47
  17.0 1.6 %reshape.295 = bf16[256,2,1024]{2,1,0:T(2,128)(2,1)} reshape(bf16[256,2048]{1,0:T(8,128)(2,1)S(1)} %reduce.1) | data formatting | bytes 2097152
  18.6 15.7 %all-to-all-start = ((bf16[256,2,1024]{2,1,0:T(2,128)(2,1)}), bf16[256,2,1024]{2,1,0:T(2,128)(2,1)S(1)}, u32[]{:S(2)}, u32[]{:S(2)}) async-start(bf16[256,2,1024]{2,1,0:T(2,128)(2,1)} %reshape.295), calls=%async_computation | async-start | bytes 2097152 | tf_op jit(solution)/shard_map/all_to_all | solution.py:47
  34.4 0.7 fusion.84
  35.2 9.9 %broadcast_add_fusion.15 = (s32[256]{0:T(256)S(1)}, s32[256]{0:T(256)S(1)}, s32[256]{0:T(256)S(1)}, s32[256]{0:T(256)S(1)}, s32[256]{0:T(256)S(1)}, /*index=5*/s...) fusion(s32[256]{0:T(256)S(1)} %copy-done.1, ...), kind=kLoop, calls=%fused_computation.114 | loop fusion | flops 4096 | bytes 17472 | tf_op jit(solution)/shard_map/add | solution.py:22
  45.1 0.1 copy.60
  45.4 0.1 copy.73
  45.6 0.1 add.717
  45.8 0.1 copy.72
  45.9 0.1 add.711
  46.1 0.1 copy.71
  46.3 0.1 add.705
  46.5 0.1 copy.70
  46.6 0.1 add.699
  46.8 0.1 copy.69
  46.9 0.1 add.693
  47.1 0.1 copy.68
  47.3 0.1 add.687
  47.5 0.1 copy.67
  47.6 0.1 add.681
  47.8 0.1 copy.66
  47.9 0.1 add.675
  48.1 0.1 copy.65
  48.3 0.1 add.669
  48.5 0.1 copy.64
  48.6 0.1 add.663
  48.8 0.1 copy.63
  48.9 0.1 add.657
  49.1 0.1 copy.62
  49.3 0.1 add.651
  49.5 0.1 copy.61
  49.8 0.1 copy.75
  50.1 0.1 copy.74
  50.3 0.1 add.723
  50.4 0.7 fusion.82
  51.1 0.6 iota_add_fusion.15
  51.7 0.6 iota_add_fusion
  52.3 0.6 iota_add_fusion.1
  53.0 0.6 iota_add_fusion.2
  53.6 0.6 iota_add_fusion.3
  54.2 0.6 iota_add_fusion.4
  54.8 0.7 iota_add_fusion.5
  55.5 0.6 iota_add_fusion.6
  56.0 0.7 iota_add_fusion.7
  56.7 0.6 iota_add_fusion.8
  57.4 0.6 iota_add_fusion.9
  58.0 0.6 iota_add_fusion.10
  58.6 0.6 iota_add_fusion.11
  59.3 0.6 iota_add_fusion.12
  59.9 0.6 iota_add_fusion.13
  60.5 0.6 iota_add_fusion.14
  61.1 3.7 %all-to-all-done = bf16[256,2,1024]{2,1,0:T(2,128)(2,1)S(1)} async-done(((bf16[256,2,1024]{2,1,0:T(2,128)(2,1)}), bf16[256,2,1024]{2,1,0:T(2,128)(2,1)S(1)}, u32[]{:S(2)}, u32[]{:S(2)}) %all-to-all-start) | async-done | bytes 1048608 | tf_op jit(solution)/shard_map/all_to_all | solution.py:47
  64.8 0.9 reshape.296
  65.7 3.4 %fusion.1 = bf16[256,1,2048]{2,0,1:T(8,128)(2,1)} fusion(bf16[256,1,2048]{2,1,0:T(2,128)(2,1)S(1)} %reshape.296, s32[256]{0:T(256)S(1)} %add.729, s32[256]{0:T(256)S(1)} %add.723, s32[256]{0:T(256)S(1)} %add.717, s32[256]{0:T(256)S(1)} %add.711, s32[256]{0:T(256)S(1)} %add.705, s32[256]{0:T(256)S(1)} %add.699, s32[256]{0:T(256)S(1)} %add.693, ...), kind=kOutput, calls=%fused_computation.3 | convolution fusion | flops 313327616 | bytes 2129920 | tf_op jit(solution)/shard_map/dot_general | solution.py:48
  69.1 2.7 %reduce.2 = bf16[256,2048]{1,0:T(8,128)(2,1)S(1)} reduce(bf16[256,1,2048]{2,0,1:T(8,128)(2,1)} %fusion.1, bf16[]{:T(256)} %broadcast.301), dimensions={1}, to_apply=%copy.77.reduce_sub_computation | reduce | bytes 2097154 | tf_op jit(solution)/shard_map/all_to_all | solution.py:49
  71.7 0.8 reshape.297
  72.5 40.4 %all_to_all.22 = bf16[256,2,1024]{2,1,0:T(2,128)(2,1)S(1)} all-to-all(bf16[256,2,1024]{2,1,0:T(2,128)(2,1)S(1)} %reshape.297), channel_id=1, replica_groups=mesh['gx'=8,'gy'=8,'gz'=4] {'gx','gy','gz'}, dimensions={0} | all-to-all | bytes 2097152 | tf_op jit(solution)/shard_map/all_to_all | solution.py:49
  113.0 0.9 reshape.298
  113.8 6.2 %reduce = bf16[256,2048]{1,0:T(8,128)(2,1)S(1)} reduce(bf16[256,1,2048]{2,1,0:T(2,128)(2,1)S(1)} %reshape.298, bf16[]{:T(256)} %constant.20), dimensions={1}, to_apply=%all_to_all.18.reduce_sub_computation | reduce | bytes 2097154 | tf_op jit(solution)/shard_map/all_to_all | solution.py:49
  120.0 1.3 %reshape.291 = bf16[1,1,1,32,16384]{4,3,2,1,0:T(8,128)(2,1)} reshape(bf16[256,2048]{1,0:T(8,128)(2,1)S(1)} %reduce) | data formatting | bytes 2097152 | tf_op jit(solution)/shard_map/reshape | solution.py:50
  (27 shorter events, 1.8 us)
Async XLA Ops:
  0.6 0.7 copy-start
  17.0 17.3 %copy-start.2 = (s32[8]{0:T(128)S(1)}, s32[8]{0:T(128)}, u32[]{:S(2)}) copy-start(s32[8]{0:T(128)} %param.11) | copy-start | bytes 100
  17.0 18.1 %copy-start.1 = (s32[256]{0:T(256)S(1)}, s32[256]{0:T(256)}, u32[]{:S(2)}) copy-start(s32[256]{0:T(256)} %param.10) | copy-start | bytes 3076
  18.6 46.2 %all-to-all-start = ((bf16[256,2,1024]{2,1,0:T(2,128)(2,1)}), bf16[256,2,1024]{2,1,0:T(2,128)(2,1)S(1)}, u32[]{:S(2)}, u32[]{:S(2)}) async-start(bf16[256,2,1024]{2,1,0:T(2,128)(2,1)} %reshape.295), calls=%async_computation | async-start | bytes 2097152 | tf_op jit(solution)/shard_map/all_to_all | solution.py:47

commit v2 on v1

v2 whole, which is shorter than its diff:
```python
import functools

import jax
import jax.numpy as jnp
from jax import lax
from jax.experimental import pallas as pl
from jax.experimental.pallas import tpu as pltpu
from jax.sharding import PartitionSpec as P

ROUNDS = 8
learn_rate = 0.01
beta_keep = 0.9
MESH = pl.DeviceIdType.MESH
TILE = (16, 128)


def zigzag(count):
    order = [0]
    for step in range(1, count // 2 + 1):
        order += sorted({step, count - step})
    return order


def kernel(
    sizes, grad_ref, hidden_hbm, weight_hbm, moment_hbm, source_ref, shift_ref,
    mixed_ref, moment_out,
    hidden, weight, moment, fresh, outgoing, arrived, ping, pong,
    in_sems, out_sems, send_sem, recv_sem, send_sem2, recv_sem2,
):
    nx, ny, nz = sizes
    devices = nx * ny * nz
    gx, gy, gz = (lax.axis_index(a) for a in ("gx", "gy", "gz"))
    me = (gx * ny + gy) * nz + gz
    cores, low_x = 2, nz // 2
    count_y, count_x = ny // 2, 2 * low_x
    core = lax.rem(gz, 2)
    x = lax.rem(gy, 2) * low_x + gz // 2
    y = gy // 2
    columns = count_x * count_y
    chunk = nx * TILE[1]

    def column_at(step):
        there_y = lax.rem(y + step // count_x, count_y)
        there_x = lax.rem(x + lax.rem(step, count_x), count_x)
        return there_y, there_x

    def device_at(there_y, there_x, there_gx, there_core):
        there_gy = there_y * 2 + there_x // low_x
        there_gz = lax.rem(there_x, low_x) * 2 + there_core
        return there_gx, there_gy, there_gz

    barrier = pltpu.get_barrier_semaphore()

    def greet(step, _):
        there_y, there_x = column_at(step)
        for dx in zigzag(nx):
            for dc in range(cores):
                target = device_at(there_y, there_x, lax.rem(gx + dx, nx), lax.rem(core + dc, 2))

                def signal():
                    pl.semaphore_signal(barrier, inc=1, device_id=target, device_id_type=MESH)

                if dx == 0 and dc == 0:
                    pl.when(step > 0)(signal)
                else:
                    signal()
        return 0

    def loads(step):
        there_y, there_x = column_at(step)
        at = pl.ds(pl.multiple_of((there_y * count_x + there_x) * chunk, chunk), chunk)
        return [
            pltpu.make_async_copy(big.at[:, at], small.at[:, at], in_sems.at[n, step])
            for n, (big, small) in enumerate(
                ((hidden_hbm, hidden), (weight_hbm, weight), (moment_hbm, moment))
            )
        ]

    def start_load(step, _):
        for copy in loads(step):
            copy.start()
        return 0

    lax.fori_loop(0, columns, start_load, 0)
    lax.fori_loop(0, columns, greet, 0)

    def tile_of(there_y, there_x, there_gx, there_core):
        return ((there_y * count_x + there_x) * nx + there_gx) * 2 + there_core

    my_tile = tile_of(y, x, gx, core)
    grad_out = grad_ref[...]

    def compute(step, _):
        there_y, there_x = column_at(step)
        base = pl.multiple_of((there_y * count_x + there_x) * chunk, chunk)
        at = pl.ds(base, chunk)
        for copy in loads(step):
            copy.wait()
        grad = jnp.dot(grad_out, hidden[:, at], preferred_element_type=jnp.float32)
        velocity = beta_keep * moment[:, at].astype(jnp.float32) + grad
        fresh[:, at] = velocity.astype(jnp.bfloat16)
        stepped = (weight[:, at].astype(jnp.float32) - learn_rate * velocity).astype(jnp.bfloat16)
        first = (there_y * count_x + there_x) * nx * 2
        for n in range(nx):
            for c in range(cores):
                outgoing[first + n * 2 + c] = stepped[
                    c * TILE[0] : (c + 1) * TILE[0], n * TILE[1] : (n + 1) * TILE[1]
                ]
        pltpu.make_async_copy(fresh.at[:, at], moment_out.at[:, at], out_sems.at[step]).start()

        @pl.when(step == 0)
        def _():
            pl.semaphore_wait(barrier, devices - 1)

        for dx in zigzag(nx):
            for dc in range(cores):
                there_gx, there_core = lax.rem(gx + dx, nx), lax.rem(core + dc, 2)
                target = device_at(there_y, there_x, there_gx, there_core)

                def send():
                    pltpu.make_async_remote_copy(
                        src_ref=outgoing.at[tile_of(there_y, there_x, there_gx, there_core)],
                        dst_ref=arrived.at[me],
                        send_sem=send_sem,
                        recv_sem=recv_sem,
                        device_id=target,
                        device_id_type=MESH,
                    ).start()

                if dx == 0 and dc == 0:
                    pl.when(step > 0)(send)
                else:
                    send()
        return 0

    lax.fori_loop(0, columns, compute, 0)
    arrived[me] = outgoing[my_tile]

    def all_of(ref, sem):
        piece = ref.at[pl.ds(0, devices - 1)]
        return pltpu.make_async_copy(piece, piece, sem)

    all_of(arrived, recv_sem).wait()

    group = 8
    mask = devices - 1
    first_off = jnp.left_shift(jnp.int32(1), shift_ref[0])

    def permute_and_mix(n, _):
        base = n * group
        for t in range(group):
            k = base + t
            one = arrived[source_ref[k]]
            two = arrived[source_ref[(k - first_off) & mask]]
            ping[k] = (one + two) * 0.5
        return 0

    lax.fori_loop(0, devices // group, permute_and_mix, 0)
    ping[pl.ds(devices, group)] = ping[pl.ds(0, group)]
    now, later = ping, pong
    for r in range(1, ROUNDS):
        off = jnp.left_shift(jnp.int32(1), shift_ref[r])

        def mix(n, _, now=now, later=later, off=off):
            base = n * group
            back = (base - off) & mask
            later[pl.ds(base, group)] = (now[pl.ds(base, group)] + now[pl.ds(back, group)]) * 0.5
            return 0

        lax.fori_loop(0, devices // group, mix, 0)
        if r < ROUNDS - 1:
            later[pl.ds(devices, group)] = later[pl.ds(0, group)]
        now, later = later, now
    done = now

    my_rows = pl.ds(pl.multiple_of(core * TILE[0], TILE[0]), TILE[0])
    my_lanes = pl.ds(pl.multiple_of(((y * count_x + x) * nx + gx) * TILE[1], TILE[1]), TILE[1])

    def give(step, _):
        there_y, there_x = column_at(step)
        for dx in zigzag(nx):
            for dc in range(cores):
                there_gx, there_core = lax.rem(gx + dx, nx), lax.rem(core + dc, 2)
                target = device_at(there_y, there_x, there_gx, there_core)
                worker = (target[0] * ny + target[1]) * nz + target[2]

                def send():
                    pltpu.make_async_remote_copy(
                        src_ref=done.at[worker],
                        dst_ref=mixed_ref.at[my_rows, my_lanes],
                        send_sem=send_sem2,
                        recv_sem=recv_sem2,
                        device_id=target,
                        device_id_type=MESH,
                    ).start()

                if dx == 0 and dc == 0:
                    pl.when(step > 0)(send)
                else:
                    send()
        return 0

    lax.fori_loop(0, columns, give, 0)
    mixed_ref[my_rows, my_lanes] = done[me]

    def drain(step, _):
        there_y, there_x = column_at(step)
        at = pl.ds(pl.multiple_of((there_y * count_x + there_x) * chunk, chunk), chunk)
        pltpu.make_async_copy(fresh.at[:, at], moment_out.at[:, at], out_sems.at[step]).wait()
        return 0

    lax.fori_loop(0, columns, drain, 0)
    all_of(arrived, send_sem).wait()
    all_of(arrived, send_sem2).wait()
    all_of(arrived, recv_sem2).wait()


def shards(sizes, hidden_acts, output_grad, weights, momentum, worker_of_slot, round_shift):
    nx, ny, nz = sizes
    devices = nx * ny * nz
    hidden = hidden_acts.reshape(hidden_acts.shape[-2:])
    grad_out = output_grad.reshape(output_grad.shape[-2:]).T
    weight = weights.reshape(weights.shape[-2:])
    moment = momentum.reshape(momentum.shape[-2:])
    rows, width = weight.shape
    slot = jnp.arange(devices, dtype=jnp.int32)
    place = (slot % nx * ny + slot // nx % ny) * nz + slot // (nx * ny)
    source = jnp.sum(
        jnp.where(worker_of_slot[None, :] == slot[:, None], place[None, :], 0), axis=1, dtype=jnp.int32
    )
    columns = devices // (2 * nx)
    tiles = (devices,) + TILE
    padded = (devices + 8,) + TILE
    vmem, smem, hbm = (
        pl.BlockSpec(memory_space=m) for m in (pltpu.VMEM, pltpu.SMEM, pltpu.HBM)
    )
    mixed, new_moment = pl.pallas_call(
        functools.partial(kernel, sizes),
        out_shape=[jax.ShapeDtypeStruct((rows, width), jnp.bfloat16)] * 2,
        in_specs=[vmem, hbm, hbm, hbm, smem, smem],
        out_specs=[vmem, hbm],
        scratch_shapes=[
            pltpu.VMEM(hidden.shape, jnp.bfloat16),
            pltpu.VMEM((rows, width), jnp.bfloat16),
            pltpu.VMEM((rows, width), jnp.bfloat16),
            pltpu.VMEM((rows, width), jnp.bfloat16),
            pltpu.VMEM(tiles, jnp.bfloat16),
            pltpu.VMEM(tiles, jnp.bfloat16),
            pltpu.VMEM(padded, jnp.bfloat16),
            pltpu.VMEM(padded, jnp.bfloat16),
            pltpu.SemaphoreType.DMA((3, columns)),
            pltpu.SemaphoreType.DMA((columns,)),
            pltpu.SemaphoreType.DMA,
            pltpu.SemaphoreType.DMA,
            pltpu.SemaphoreType.DMA,
            pltpu.SemaphoreType.DMA,
        ],
        compiler_params=pltpu.CompilerParams(
            collective_id=0, has_side_effects=True, vmem_limit_bytes=56 * 1024 * 1024
        ),
        name="step",
    )(grad_out, hidden, weight, moment, source, round_shift)
    return mixed.reshape(weights.shape), new_moment.reshape(momentum.shape)


def solution(mesh):
    sizes = tuple(mesh.shape[a] for a in ("gx", "gy", "gz"))
    placed = (
        P("gz", "gy", "gx", None, None),
        P("gz", "gy", "gx", None, None),
        P("gz", "gy", "gx", None, None),
        P("gz", "gy", "gx", None, None),
        P(),
        P(),
    )
    return jax.shard_map(
        functools.partial(shards, sizes),
        mesh=mesh,
        in_specs=placed,
        out_specs=(P("gx", "gy", "gz", None, None), P("gz", "gy", "gx", None, None)),
        check_vma=False,
    )
```

time: 122 us -> 81.7 us (0.67)
  Pallas kernels: 0 us -> 75 us
  blocking collectives: 40.4 us -> 0 us
  other arithmetic: 35.5 us -> 1.37 us
  starting transfers between devices: 15.7 us -> 0 us
  local copies, waits for them, and re-layouts: 15.1 us -> 4.52 us
  matrix products: 9.96 us -> 0 us
  waiting for transfers between devices: 3.69 us -> 0 us
    pallas_call x0 -> x1, Pallas kernels: none -> 75 us  [shards(): pl.pallas_call(functools.partial(kernel, sizes), out_shape=[jax.ShapeDtyp...]
    all_to_all x1 -> x0, blocking collectives: 40.4 us -> none  [shards(): back = lax.all_to_all(mixed, AXES, split_axis=0, concat_axis=0, tiled=True)]
    add x17 -> x1, other arithmetic: 19.8 us -> 0.01 us  [shards(): place = (slot % nx * ny + slot // nx % ny) * nz + slot // (nx * ny)]
    all_to_all x3 -> x0, other arithmetic: 15.7 us -> none  [the longest x2 8.83 us: shards(): back = lax.all_to_all(mixed, AXES, split_axis=0, concat_axis=0, tiled=True)]
    all_to_all x1 -> x0, starting transfers between devices: 15.7 us -> none  [shards(): lax.all_to_all(pieces, AXES, split_axis=0, concat_axis=0, tiled=True)]
    dot_general x2 -> x0, matrix products: 9.96 us -> none  [the longest x1 6.59 us: shards(): lax.dot_general(grad_out, hidden, (((0,), (0,)), ((), ())), preferred_ele...]
    add x48 -> x0, local copies, waits for them, and re-layouts: 5.29 us -> none  [mixing(): first += held[None, :] + low[m] - index[:, None] & workers - 1 == 0]
    all_to_all x1 -> x0, waiting for transfers between devices: 3.69 us -> none  [shards(): lax.all_to_all(pieces, AXES, split_axis=0, concat_axis=0, tiled=True)]
  transfers between devices with their start and end apart: 1 -> 0, of which waited for: 1 -> 0; matrix products, arithmetic and copies ran while one was open for 22% -> 0% of each run, Pallas kernels for 0% -> 0%
where the time goes in v2:
time: 81.7 us; the launch traced here: 81.5 us
  Pallas kernels  75 us (92%)
  local copies, waits for them, and re-layouts  4.52 us (6%)
  other arithmetic  1.37 us (2%)
    pallas_call x1, Pallas kernels, shards(): pl.pallas_call(functools.partial(kernel, sizes), out_shape=[jax.ShapeDtyp...  75 us
    unnamed x2, local copies, waits for them, and re-layouts  4.52 us

profile of v2, /device:TPU:1, one launch (start us, length us, event | category | flops | bytes accessed | tf_op | source)
XLA Modules:
  0.0 81.5 jit_solution(3356256834344360651)
XLA Ops:
  0.6 1.4 %select_reduce_fusion.source_ref = s32[256]{0:T(256)} fusion(s32[256]{0:T(256)S(1)} %fusion.5, s32[256]{0:T(256)} %param.10), kind=kLoop, calls=%fused_computation | loop fusion | flops 196352 | bytes 3072 | tf_op jit(solution)/shard_map/reduce_sum | solution.py:228
  2.0 75.0 %step.1 = (bf16[32,16384]{1,0:T(8,128)(2,1)}, bf16[32,16384]{1,0:T(8,128)(2,1)}) custom-call(bf16[32,256]{1,0:T(8,128)(2,1)} %bitcast.13, bf16[256,16384]{1,0:T(8,128)(2,1)} %bitcast.8, bf16[32,16384]{1,0:T(8,128)(2,1)} %bitcast.11, bf16[32,16384]{1,0:T(8,128)(2,1)} %bitcast.12, s32[256]{0:T(256)} %select_reduce_fusion.source_ref, s32[8]{0:T(128)} %shift_ref.1), custom_call_target="tpu_custom_call" | custom-call | tf_op jit(solution)/shard_map/step/pallas_call | solution.py:237
  77.0 2.3 %copy.10 = bf16[1,1,1,32,16384]{4,3,2,1,0:T(8,128)(2,1)} copy(bf16[1,1,1,32,16384]{4,3,2,1,0:T(8,128)(2,1)} %bitcast.10) | data formatting | bytes 2097152
  79.2 2.3 %copy.11 = bf16[1,1,1,32,16384]{4,3,2,1,0:T(8,128)(2,1)} copy(bf16[1,1,1,32,16384]{4,3,2,1,0:T(8,128)(2,1)} %bitcast.9) | data formatting | bytes 2097152
  (1 shorter events, 0.0 us)

commit v3 on v2

v3 whole, which is shorter than its diff:
```python
import functools

import jax
import jax.numpy as jnp
from jax import lax
from jax.experimental import pallas as pl
from jax.experimental.pallas import tpu as pltpu
from jax.sharding import PartitionSpec as P

ROUNDS = 8
learn_rate = 0.01
beta_keep = 0.9
MESH = pl.DeviceIdType.MESH
TILE = (16, 128)


def zigzag(count):
    order = [0]
    for step in range(1, count // 2 + 1):
        order += sorted({step, count - step})
    return order


def kernel(
    sizes, grad_hbm, hidden_hbm, weight_hbm, moment_hbm, held_hbm, shift_hbm,
    mixed_ref, moment_out,
    hidden, weight, moment, outgoing, arrived, ping, pong, table, source_ref,
    grad_ref, held_ref, shift_ref, in_sems, table_sem, small_sems, send_sem, recv_sem, send_sem2, recv_sem2,
):
    nx, ny, nz = sizes
    devices = nx * ny * nz
    gx, gy, gz = (lax.axis_index(a) for a in ("gx", "gy", "gz"))
    me = (gx * ny + gy) * nz + gz
    cores, low_x = 2, nz // 2
    count_y, count_x = ny // 2, 2 * low_x
    core = lax.rem(gz, 2)
    x = lax.rem(gy, 2) * low_x + gz // 2
    y = gy // 2
    columns = count_x * count_y
    chunk = nx * TILE[1]

    def column_at(step):
        there_y = lax.rem(y + step // count_x, count_y)
        there_x = lax.rem(x + lax.rem(step, count_x), count_x)
        return there_y, there_x

    def device_at(there_y, there_x, there_gx, there_core):
        there_gy = there_y * 2 + there_x // low_x
        there_gz = lax.rem(there_x, low_x) * 2 + there_core
        return there_gx, there_gy, there_gz

    barrier = pltpu.get_barrier_semaphore()

    def greet(step, _):
        there_y, there_x = column_at(lax.rem(step + columns // 2, columns))
        for dx in reversed(zigzag(nx)):
            for dc in range(cores):
                target = device_at(there_y, there_x, lax.rem(gx + dx, nx), lax.rem(core + dc, 2))

                def signal():
                    pl.semaphore_signal(barrier, inc=1, device_id=target, device_id_type=MESH)

                if dx == 0 and dc == 0:
                    pl.when(step != columns // 2)(signal)
                else:
                    signal()
        return 0

    def loads(step):
        there_y, there_x = column_at(step)
        at = pl.ds(pl.multiple_of((there_y * count_x + there_x) * chunk, chunk), chunk)
        return [
            pltpu.make_async_copy(big.at[:, at], small.at[:, at], in_sems.at[n, step])
            for n, (big, small) in enumerate(
                ((hidden_hbm, hidden), (weight_hbm, weight), (moment_hbm, moment))
            )
        ]

    def start_load(step, _):
        for copy in loads(step):
            copy.start()
        return 0

    small_loads = [
        pltpu.make_async_copy(far, near, small_sems.at[n])
        for n, (far, near) in enumerate(
            ((grad_hbm, grad_ref), (held_hbm, held_ref), (shift_hbm, shift_ref))
        )
    ]
    for copy in small_loads:
        copy.start()
    start_load(0, 0)
    with jax.named_scope('s1_greet'):
        lax.fori_loop(0, columns, greet, 0)
    lax.fori_loop(1, columns, start_load, 0)

    def tile_of(there_y, there_x, there_gx, there_core):
        return ((there_y * count_x + there_x) * nx + there_gx) * 2 + there_core

    my_tile = tile_of(y, x, gx, core)
    for copy in small_loads:
        copy.wait()
    grad_out = grad_ref[...]

    def send_tiles(step, there_core):
        there_y, there_x = column_at(step)
        for dx in zigzag(nx):
            there_gx = lax.rem(gx + dx, nx)
            target = device_at(there_y, there_x, there_gx, there_core)

            def send():
                pltpu.make_async_remote_copy(
                    src_ref=outgoing.at[tile_of(there_y, there_x, there_gx, there_core)],
                    dst_ref=arrived.at[me],
                    send_sem=send_sem,
                    recv_sem=recv_sem,
                    device_id=target,
                    device_id_type=MESH,
                ).start()

            if dx == 0:
                pl.when((step > 0) | (core != there_core))(send)
            else:
                send()

    def compute(step, _):
        there_y, there_x = column_at(step)
        base = pl.multiple_of((there_y * count_x + there_x) * chunk, chunk)
        at = pl.ds(base, chunk)
        for copy in loads(step):
            copy.wait()
        grad = jnp.dot(grad_out, hidden[:, at], preferred_element_type=jnp.float32)
        velocity = beta_keep * moment[:, at].astype(jnp.float32) + grad
        moment_out[:, at] = velocity.astype(jnp.bfloat16)
        stepped = (weight[:, at].astype(jnp.float32) - learn_rate * velocity).astype(jnp.bfloat16)
        first = (there_y * count_x + there_x) * nx * 2
        for n in range(nx):
            for c in range(cores):
                outgoing[first + n * 2 + c] = stepped[
                    c * TILE[0] : (c + 1) * TILE[0], n * TILE[1] : (n + 1) * TILE[1]
                ]

        @pl.when(step == 0)
        def _():
            with jax.named_scope('s2_barrier'):
                pl.semaphore_wait(barrier, devices - 1)

        send_tiles(step, 0)
        return 0

    with jax.named_scope('s2_compute'):
        lax.fori_loop(0, columns, compute, 0)

    def second_wave(step, _):
        send_tiles(step, 1)
        return 0

    with jax.named_scope('s2_wave'):
        lax.fori_loop(0, columns, second_wave, 0)
    arrived[me] = outgoing[my_tile]

    held = jnp.broadcast_to(held_ref[...], (8, devices)).T[:, :1]
    slot = lax.broadcasted_iota(jnp.int32, (devices, devices), 0)
    worker = lax.broadcasted_iota(jnp.int32, (devices, devices), 1)
    place = (lax.rem(slot, nx) * ny + lax.rem(slot // nx, ny)) * nz + slot // (nx * ny)
    table[...] = jnp.sum(jnp.where(held == worker, place, 0), axis=0, keepdims=True) & (devices - 1)
    to_scalars = pltpu.make_async_copy(table, source_ref, table_sem)
    to_scalars.start()
    to_scalars.wait()

    def all_of(ref, sem):
        piece = ref.at[pl.ds(0, devices - 1)]
        return pltpu.make_async_copy(piece, piece, sem)

    with jax.named_scope('s3_recv1'):
        all_of(arrived, recv_sem).wait()

    group = 8
    wide = 16
    mask = devices - 1
    first_off = jnp.left_shift(jnp.int32(1), shift_ref[0])

    def permute_and_mix(n, _):
        base = n * group
        for t in range(group):
            k = base + t
            one = arrived[source_ref[0, k]]
            two = arrived[source_ref[0, (k - first_off) & mask]]
            ping[k] = (one + two) * 0.5
        return 0

    with jax.named_scope('s4_perm'):
        lax.fori_loop(0, devices // group, permute_and_mix, 0)
    ping[pl.ds(devices, group)] = ping[pl.ds(0, group)]
    now, later = ping, pong
    for r in range(1, ROUNDS):
        off = jnp.left_shift(jnp.int32(1), shift_ref[r])

        def mix(n, _, now=now, later=later, off=off):
            for part in range(wide // group):
                base = n * wide + part * group
                back = (base - off) & mask
                later[pl.ds(base, group)] = (
                    now[pl.ds(base, group)] + now[pl.ds(back, group)]
                ) * 0.5
            return 0

        with jax.named_scope('s5_mix'):
            lax.fori_loop(0, devices // wide, mix, 0)
        if r < ROUNDS - 1:
            later[pl.ds(devices, group)] = later[pl.ds(0, group)]
        now, later = later, now
    done = now

    my_rows = pl.ds(pl.multiple_of(core * TILE[0], TILE[0]), TILE[0])
    my_lanes = pl.ds(pl.multiple_of(((y * count_x + x) * nx + gx) * TILE[1], TILE[1]), TILE[1])

    def give(step, _):
        there_y, there_x = column_at(step)
        for dx in zigzag(nx):
            for dc in range(cores):
                there_gx, there_core = lax.rem(gx + dx, nx), lax.rem(core + dc, 2)
                target = device_at(there_y, there_x, there_gx, there_core)
                worker = (target[0] * ny + target[1]) * nz + target[2]

                def send():
                    pltpu.make_async_remote_copy(
                        src_ref=done.at[worker],
                        dst_ref=mixed_ref.at[my_rows, my_lanes],
                        send_sem=send_sem2,
                        recv_sem=recv_sem2,
                        device_id=target,
                        device_id_type=MESH,
                    ).start()

                if dx == 0 and dc == 0:
                    pl.when(step > 0)(send)
                else:
                    send()
        return 0

    with jax.named_scope('s6_give'):
        lax.fori_loop(0, columns, give, 0)
    mixed_ref[my_rows, my_lanes] = done[me]

    with jax.named_scope('s7_send1'):
        all_of(arrived, send_sem).wait()
    with jax.named_scope('s8_send2'):
        all_of(arrived, send_sem2).wait()
    with jax.named_scope('s9_recv2'):
        all_of(arrived, recv_sem2).wait()


def put_kernel(*refs):
    count = (len(refs) - 1) // 2
    sources, targets, sems = refs[:count], refs[count : 2 * count], refs[-1]
    parts = sems.shape[1]
    copies = []
    for n in range(count):
        width = sources[n].shape[1] // parts
        for p in range(parts):
            at = pl.ds(p * width, width)
            copies.append(
                pltpu.make_async_copy(sources[n].at[:, at], targets[n].at[:, at], sems.at[n, p])
            )
    for copy in copies:
        copy.start()
    for copy in copies:
        copy.wait()


def put(*arrays):
    parts = 4
    held = [pltpu.with_memory_space_constraint(a, pltpu.VMEM) for a in arrays]
    return pl.pallas_call(
        put_kernel,
        out_shape=[pltpu.HBM(a.shape, a.dtype) for a in arrays],
        in_specs=[pl.BlockSpec(memory_space=pltpu.VMEM)] * len(arrays),
        out_specs=[pl.BlockSpec(memory_space=pltpu.HBM)] * len(arrays),
        scratch_shapes=[pltpu.SemaphoreType.DMA((len(arrays), parts))],
        name="put",
    )(*held)


def shards(sizes, hidden_acts, output_grad, weights, momentum, worker_of_slot, round_shift):
    nx, ny, nz = sizes
    devices = nx * ny * nz
    hidden = hidden_acts.reshape(hidden_acts.shape[-2:])
    grad_out = output_grad.reshape(output_grad.shape[-2:]).T
    weight = weights.reshape(weights.shape[-2:])
    moment = momentum.reshape(momentum.shape[-2:])
    rows, width = weight.shape
    columns = devices // (2 * nx)
    tiles = (devices,) + TILE
    padded = (devices + 8,) + TILE
    inputs = [
        pltpu.with_memory_space_constraint(a, pltpu.HBM)
        for a in (grad_out, hidden, weight, moment, worker_of_slot.reshape(1, -1), round_shift)
    ]
    vmem, hbm = (pl.BlockSpec(memory_space=m) for m in (pltpu.VMEM, pltpu.HBM))
    mixed, new_moment = pl.pallas_call(
        functools.partial(kernel, sizes),
        out_shape=[pltpu.VMEM((rows, width), jnp.bfloat16)] * 2,
        in_specs=[hbm] * len(inputs),
        out_specs=[vmem, vmem],
        scratch_shapes=[
            pltpu.VMEM(hidden.shape, jnp.bfloat16),
            pltpu.VMEM((rows, width), jnp.bfloat16),
            pltpu.VMEM((rows, width), jnp.bfloat16),
            pltpu.VMEM(tiles, jnp.bfloat16),
            pltpu.VMEM(tiles, jnp.bfloat16),
            pltpu.VMEM(padded, jnp.bfloat16),
            pltpu.VMEM(padded, jnp.bfloat16),
            pltpu.VMEM((1, devices), jnp.int32),
            pltpu.SMEM((1, devices), jnp.int32),
            pltpu.VMEM(grad_out.shape, jnp.bfloat16),
            pltpu.VMEM((1, devices), jnp.int32),
            pltpu.SMEM((ROUNDS,), jnp.int32),
            pltpu.SemaphoreType.DMA((3, columns)),
            pltpu.SemaphoreType.DMA,
            pltpu.SemaphoreType.DMA((3,)),
            pltpu.SemaphoreType.DMA,
            pltpu.SemaphoreType.DMA,
            pltpu.SemaphoreType.DMA,
            pltpu.SemaphoreType.DMA,
        ],
        compiler_params=pltpu.CompilerParams(
            collective_id=0, has_side_effects=True, vmem_limit_bytes=40 * 1024 * 1024
        ),
        name="step",
    )(*inputs)
    mixed, new_moment = put(mixed, new_moment)
    return mixed.reshape(weights.shape), new_moment.reshape(momentum.shape)


def solution(mesh):
    sizes = tuple(mesh.shape[a] for a in ("gx", "gy", "gz"))
    placed = (
        P("gz", "gy", "gx", None, None),
        P("gz", "gy", "gx", None, None),
        P("gz", "gy", "gx", None, None),
        P("gz", "gy", "gx", None, None),
        P(),
        P(),
    )
    return jax.shard_map(
        functools.partial(shards, sizes),
        mesh=mesh,
        in_specs=placed,
        out_specs=(P("gx", "gy", "gz", None, None), P("gz", "gy", "gx", None, None)),
        check_vma=False,
    )
```

time: 81.7 us -> 64 us (0.78)
  Pallas kernels: 75 us -> 63.3 us
  local copies, waits for them, and re-layouts: 4.52 us -> 0 us
  other arithmetic: 1.37 us -> 0 us
    pallas_call x1 -> x2, Pallas kernels: 75 us -> 63.3 us  [the longest x1 61.9 us: shards(): pl.pallas_call(functools.partial(kernel, sizes), out_shape=[pltpu.VMEM((r...]
    unnamed x2 -> x0, local copies, waits for them, and re-layouts: 4.52 us -> none
    reduce_sum x1 -> x0, other arithmetic: 1.36 us -> none  [shards(): jnp.sum(jnp.where(worker_of_slot[None, :] == slot[:, None], place[None, :...]
where the time goes in v3:
time: 64 us; the launch traced here: 63.9 us
  Pallas kernels  63.3 us (99%)
  between operations  0.64 us (1%)
    pallas_call x1, Pallas kernels, shards(): pl.pallas_call(functools.partial(kernel, sizes), out_shape=[pltpu.VMEM((r...  61.9 us
    pallas_call x1, Pallas kernels, put(): pl.pallas_call(put_kernel, out_shape=[pltpu.HBM(a.shape, a.dtype) for a i...  1.38 us

profile of v3, /device:TPU:1, one launch (start us, length us, event | category | flops | bytes accessed | tf_op | source)
XLA Modules:
  0.0 63.9 jit_solution(8180819135881918522)
XLA Ops:
  0.6 61.9 %step.1 = (bf16[32,16384]{1,0:T(8,128)(2,1)S(1)}, bf16[32,16384]{1,0:T(8,128)(2,1)S(1)}) custom-call(bf16[32,256]{1,0:T(8,128)(2,1)} %bitcast.12, bf16[256,16384]{1,0:T(8,128)(2,1)} %bitcast.9, bf16[32,16384]{1,0:T(8,128)(2,1)} %bitcast.10, bf16[32,16384]{1,0:T(8,128)(2,1)} %bitcast.11, s32[1,256]{1,0:T(1,128)} %bitcast.13, s32[8]{0:T(128)} %shift_hbm.1), custom_call_target="tpu_custom_call" | custom-call | tf_op jit(solution)/shard_map/step/pallas_call | solution.py:301
  62.6 1.4 %put.1 = (bf16[32,16384]{1,0:T(8,128)(2,1)}, bf16[32,16384]{1,0:T(8,128)(2,1)}) custom-call(bf16[32,16384]{1,0:T(8,128)(2,1)S(1)} %get-tuple-element.6.refs_0_, bf16[32,16384]{1,0:T(8,128)(2,1)S(1)} %get-tuple-element.7.refs_1_), custom_call_target="tpu_custom_call" | custom-call | tf_op jit(solution)/shard_map/put/pallas_call | solution.py:275

commit v4 on v3

--- a/solution.py
+++ b/solution.py
@@ -25,7 +25,7 @@
     sizes, grad_hbm, hidden_hbm, weight_hbm, moment_hbm, held_hbm, shift_hbm,
     mixed_ref, moment_out,
     hidden, weight, moment, outgoing, arrived, ping, pong, table, source_ref,
-    grad_ref, held_ref, shift_ref, in_sems, table_sem, small_sems, send_sem, recv_sem, send_sem2, recv_sem2,
+    grad_ref, held_ref, shift_ref, ready, in_sems, table_sem, small_sems, send_sem, recv_sem, send_sem2, recv_sem2,
 ):
     nx, ny, nz = sizes
     devices = nx * ny * nz
@@ -51,20 +51,29 @@
 
     barrier = pltpu.get_barrier_semaphore()
 
-    def greet(step, _):
-        there_y, there_x = column_at(lax.rem(step + columns // 2, columns))
-        for dx in reversed(zigzag(nx)):
+    def tell(semaphore, target):
+        pl.semaphore_signal(semaphore, inc=1, device_id=target, device_id_type=MESH)
+
+    def greet_plane(step, _):
+        tell(barrier, device_at(*column_at(step), gx, core))
+        return 0
+
+    def greet():
+        for dx in zigzag(nx):
             for dc in range(cores):
-                target = device_at(there_y, there_x, lax.rem(gx + dx, nx), lax.rem(core + dc, 2))
-
-                def signal():
-                    pl.semaphore_signal(barrier, inc=1, device_id=target, device_id_type=MESH)
-
-                if dx == 0 and dc == 0:
-                    pl.when(step != columns // 2)(signal)
-                else:
-                    signal()
-        return 0
+                if dx or dc:
+                    tell(barrier, device_at(y, x, lax.rem(gx + dx, nx), lax.rem(core + dc, 2)))
+        lax.fori_loop(1, columns, greet_plane, 0)
+
+    def vouch(step, _):
+        back_y = lax.rem(count_y - step // count_x, count_y)
+        back_x = lax.rem(count_x - lax.rem(step, count_x), count_x)
+        tell(ready.at[back_y * count_x + back_x], device_at(*column_at(step), gx, core))
+        return 0
+
+    def meet():
+        pl.semaphore_wait(barrier, nx * cores - 1 + columns - 1)
+        lax.fori_loop(1, columns, vouch, 0)
 
     def loads(step):
         there_y, there_x = column_at(step)
@@ -89,10 +98,9 @@
     ]
     for copy in small_loads:
         copy.start()
-    start_load(0, 0)
-    with jax.named_scope('s1_greet'):
-        lax.fori_loop(0, columns, greet, 0)
-    lax.fori_loop(1, columns, start_load, 0)
+    with jax.named_scope("s1_greet"):
+        greet()
+        lax.fori_loop(0, columns, start_load, 0)
 
     def tile_of(there_y, there_x, there_gx, there_core):
         return ((there_y * count_x + there_x) * nx + there_gx) * 2 + there_core
@@ -140,14 +148,15 @@
                     c * TILE[0] : (c + 1) * TILE[0], n * TILE[1] : (n + 1) * TILE[1]
                 ]
 
-        @pl.when(step == 0)
+        @pl.when(step > 0)
         def _():
-            with jax.named_scope('s2_barrier'):
-                pl.semaphore_wait(barrier, devices - 1)
+            pl.semaphore_wait(ready.at[step], 1)
 
         send_tiles(step, 0)
         return 0
 
+    with jax.named_scope("s2_barrier"):
+        meet()
     with jax.named_scope('s2_compute'):
         lax.fori_loop(0, columns, compute, 0)
 
@@ -216,8 +225,8 @@
     my_lanes = pl.ds(pl.multiple_of(((y * count_x + x) * nx + gx) * TILE[1], TILE[1]), TILE[1])
 
     def give(step, _):
-        there_y, there_x = column_at(step)
-        for dx in zigzag(nx):
+        there_y, there_x = column_at(columns - 1 - step)
+        for dx in reversed(zigzag(nx)):
             for dc in range(cores):
                 there_gx, there_core = lax.rem(gx + dx, nx), lax.rem(core + dc, 2)
                 target = device_at(there_y, there_x, there_gx, there_core)
@@ -234,7 +243,7 @@
                     ).start()
 
                 if dx == 0 and dc == 0:
-                    pl.when(step > 0)(send)
+                    pl.when(step < columns - 1)(send)
                 else:
                     send()
         return 0
@@ -316,6 +325,7 @@
             pltpu.VMEM(grad_out.shape, jnp.bfloat16),
             pltpu.VMEM((1, devices), jnp.int32),
             pltpu.SMEM((ROUNDS,), jnp.int32),
+            pltpu.SemaphoreType.REGULAR((columns,)),
             pltpu.SemaphoreType.DMA((3, columns)),
             pltpu.SemaphoreType.DMA,
             pltpu.SemaphoreType.DMA((3,)),

time: 64 us -> 62.5 us (0.977)
  Pallas kernels: 63.3 us -> 61.7 us
    pallas_call x1, Pallas kernels: 61.9 us -> 60.3 us  [shards(): pl.pallas_call(functools.partial(kernel, sizes), out_shape=[pltpu.VMEM((r...]
where the time goes in v4:
time: 62.5 us; the launch traced here: 62.3 us
  Pallas kernels  61.7 us (99%)
  between operations  0.64 us (1%)
    pallas_call x1, Pallas kernels, shards(): pl.pallas_call(functools.partial(kernel, sizes), out_shape=[pltpu.VMEM((r...  60.3 us
    pallas_call x1, Pallas kernels, put(): pl.pallas_call(put_kernel, out_shape=[pltpu.HBM(a.shape, a.dtype) for a i...  1.38 us

profile of v4, /device:TPU:1, one launch (start us, length us, event | category | flops | bytes accessed | tf_op | source)
XLA Modules:
  0.0 62.3 jit_solution(2613337458130539894)
XLA Ops:
  0.6 60.3 %step.1 = (bf16[32,16384]{1,0:T(8,128)(2,1)S(1)}, bf16[32,16384]{1,0:T(8,128)(2,1)S(1)}) custom-call(bf16[32,256]{1,0:T(8,128)(2,1)} %bitcast.12, bf16[256,16384]{1,0:T(8,128)(2,1)} %bitcast.9, bf16[32,16384]{1,0:T(8,128)(2,1)} %bitcast.10, bf16[32,16384]{1,0:T(8,128)(2,1)} %bitcast.11, s32[1,256]{1,0:T(1,128)} %bitcast.13, s32[8]{0:T(128)} %shift_hbm.1), custom_call_target="tpu_custom_call" | custom-call | tf_op jit(solution)/shard_map/step/pallas_call | solution.py:310
  61.0 1.4 %put.1 = (bf16[32,16384]{1,0:T(8,128)(2,1)}, bf16[32,16384]{1,0:T(8,128)(2,1)}) custom-call(bf16[32,16384]{1,0:T(8,128)(2,1)S(1)} %get-tuple-element.6.refs_0_, bf16[32,16384]{1,0:T(8,128)(2,1)S(1)} %get-tuple-element.7.refs_1_), custom_call_target="tpu_custom_call" | custom-call | tf_op jit(solution)/shard_map/put/pallas_call | solution.py:284

commit v5 on v4

--- a/solution.py
+++ b/solution.py
@@ -39,6 +39,15 @@
     columns = count_x * count_y
     chunk = nx * TILE[1]
 
+    def spread(turn):
+        along_y = turn * count_x
+        along_x = turn - (count_y - 1)
+        rest = turn - (count_y + count_x - 1)
+        others = (1 + rest // (count_x - 1)) * count_x + 1 + lax.rem(rest, count_x - 1)
+        return jnp.where(
+            turn < count_y, along_y, jnp.where(turn < count_y + count_x - 1, along_x, others)
+        )
+
     def column_at(step):
         there_y = lax.rem(y + step // count_x, count_y)
         there_x = lax.rem(x + lax.rem(step, count_x), count_x)
@@ -54,26 +63,38 @@
     def tell(semaphore, target):
         pl.semaphore_signal(semaphore, inc=1, device_id=target, device_id_type=MESH)
 
-    def greet_plane(step, _):
-        tell(barrier, device_at(*column_at(step), gx, core))
-        return 0
+    def peer(dy, dx):
+        return device_at(lax.rem(y + dy, count_y), lax.rem(x + dx, count_x), gx, core)
 
     def greet():
         for dx in zigzag(nx):
             for dc in range(cores):
                 if dx or dc:
                     tell(barrier, device_at(y, x, lax.rem(gx + dx, nx), lax.rem(core + dc, 2)))
-        lax.fori_loop(1, columns, greet_plane, 0)
-
-    def vouch(step, _):
-        back_y = lax.rem(count_y - step // count_x, count_y)
-        back_x = lax.rem(count_x - lax.rem(step, count_x), count_x)
-        tell(ready.at[back_y * count_x + back_x], device_at(*column_at(step), gx, core))
-        return 0
+        for dy in range(1, count_y):
+            tell(barrier, peer(dy, 0))
+        for dx in range(1, count_x):
+            tell(barrier, peer(0, dx))
+
+    def vouch_to(dy, dx, about_y):
+        seen_y = (count_y - dy + about_y) % count_y
+        tell(ready.at[seen_y * count_x + (count_x - dx) % count_x], peer(dy, dx))
 
     def meet():
-        pl.semaphore_wait(barrier, nx * cores - 1 + columns - 1)
-        lax.fori_loop(1, columns, vouch, 0)
+        pl.semaphore_wait(barrier, nx * cores - 1 + count_y - 1 + count_x - 1)
+        for dy in range(1, count_y):
+            vouch_to(dy, 0, 0)
+        for dx in range(1, count_x):
+            vouch_to(0, dx, 0)
+
+    def await_column(step):
+        pl.semaphore_wait(ready.at[step], 1)
+        for dy in range(1, count_y):
+
+            @pl.when(step == dy * count_x)
+            def _():
+                for dx in range(1, count_x):
+                    vouch_to(0, dx, dy)
 
     def loads(step):
         there_y, there_x = column_at(step)
@@ -85,8 +106,8 @@
             )
         ]
 
-    def start_load(step, _):
-        for copy in loads(step):
+    def start_load(turn, _):
+        for copy in loads(spread(turn)):
             copy.start()
         return 0
 
@@ -131,7 +152,8 @@
             else:
                 send()
 
-    def compute(step, _):
+    def compute(turn, _):
+        step = spread(turn)
         there_y, there_x = column_at(step)
         base = pl.multiple_of((there_y * count_x + there_x) * chunk, chunk)
         at = pl.ds(base, chunk)
@@ -150,7 +172,7 @@
 
         @pl.when(step > 0)
         def _():
-            pl.semaphore_wait(ready.at[step], 1)
+            await_column(step)
 
         send_tiles(step, 0)
         return 0
@@ -224,31 +246,60 @@
     my_rows = pl.ds(pl.multiple_of(core * TILE[0], TILE[0]), TILE[0])
     my_lanes = pl.ds(pl.multiple_of(((y * count_x + x) * nx + gx) * TILE[1], TILE[1]), TILE[1])
 
+    corner = [(0, 0), (0, 1), (0, count_x - 1), (1, 0), (count_y - 1, 0)][:5]
+    corner = sorted(set(corner))
+    planes = min(4, nx)
+    early = len(corner) * planes * cores
+
+    def give_to(there_y, there_x, there_gx, there_core):
+        target = device_at(there_y, there_x, there_gx, there_core)
+        worker = (target[0] * ny + target[1]) * nz + target[2]
+        pltpu.make_async_remote_copy(
+            src_ref=done.at[worker],
+            dst_ref=mixed_ref.at[my_rows, my_lanes],
+            send_sem=send_sem2,
+            recv_sem=recv_sem2,
+            device_id=target,
+            device_id_type=MESH,
+        ).start()
+
+    def give_early(n, _):
+        turn = lax.rem(n + me, early)
+        there_core, there_gx = lax.rem(turn, cores), lax.rem(turn // cores, planes)
+        column = turn // (cores * planes)
+        there_y = there_x = jnp.int32(0)
+        for c, (cy, cx) in enumerate(corner):
+            there_y = jnp.where(column == c, cy, there_y)
+            there_x = jnp.where(column == c, cx, there_x)
+        myself = (there_y == y) & (there_x == x) & (there_gx == gx) & (there_core == core)
+
+        @pl.when(jnp.logical_not(myself))
+        def _():
+            give_to(there_y, there_x, there_gx, there_core)
+
+        return 0
+
     def give(step, _):
         there_y, there_x = column_at(columns - 1 - step)
+        near = functools.reduce(
+            jnp.logical_or, [(there_y == cy) & (there_x == cx) for cy, cx in corner]
+        )
         for dx in reversed(zigzag(nx)):
+            there_gx = lax.rem(gx + dx, nx)
             for dc in range(cores):
-                there_gx, there_core = lax.rem(gx + dx, nx), lax.rem(core + dc, 2)
-                target = device_at(there_y, there_x, there_gx, there_core)
-                worker = (target[0] * ny + target[1]) * nz + target[2]
-
-                def send():
-                    pltpu.make_async_remote_copy(
-                        src_ref=done.at[worker],
-                        dst_ref=mixed_ref.at[my_rows, my_lanes],
-                        send_sem=send_sem2,
-                        recv_sem=recv_sem2,
-                        device_id=target,
-                        device_id_type=MESH,
-                    ).start()
-
+                there_core = lax.rem(core + dc, 2)
+                skip = near & (there_gx < planes)
                 if dx == 0 and dc == 0:
-                    pl.when(step < columns - 1)(send)
-                else:
-                    send()
-        return 0
-
-    with jax.named_scope('s6_give'):
+                    skip = skip | (step == columns - 1)
+
+                @pl.when(jnp.logical_not(skip))
+                def _():
+                    give_to(there_y, there_x, there_gx, there_core)
+
+        return 0
+
+    with jax.named_scope("s6_give"):
+        lax.fori_loop(0, early, give_early, 0)
         lax.fori_loop(0, columns, give, 0)
     mixed_ref[my_rows, my_lanes] = done[me]
 

time: 62.5 us -> 59.9 us (0.958)
  Pallas kernels: 61.7 us -> 58.7 us
    pallas_call x1, Pallas kernels: 60.3 us -> 57.3 us  [shards(): pl.pallas_call(functools.partial(kernel, sizes), out_shape=[pltpu.VMEM((r...]
where the time goes in v5:
time: 59.9 us; the launch traced here: 59.3 us
  Pallas kernels  58.7 us (98%)
  between operations  0.64 us (1%)
    pallas_call x1, Pallas kernels, shards(): pl.pallas_call(functools.partial(kernel, sizes), out_shape=[pltpu.VMEM((r...  57.3 us
    pallas_call x1, Pallas kernels, put(): pl.pallas_call(put_kernel, out_shape=[pltpu.HBM(a.shape, a.dtype) for a i...  1.38 us

profile of v5, /device:TPU:1, one launch (start us, length us, event | category | flops | bytes accessed | tf_op | source)
XLA Modules:
  0.0 59.3 jit_solution(6720045032362369830)
XLA Ops:
  0.6 57.3 %step.1 = (bf16[32,16384]{1,0:T(8,128)(2,1)S(1)}, bf16[32,16384]{1,0:T(8,128)(2,1)S(1)}) custom-call(bf16[32,256]{1,0:T(8,128)(2,1)} %bitcast.12, bf16[256,16384]{1,0:T(8,128)(2,1)} %bitcast.9, bf16[32,16384]{1,0:T(8,128)(2,1)} %bitcast.10, bf16[32,16384]{1,0:T(8,128)(2,1)} %bitcast.11, s32[1,256]{1,0:T(1,128)} %bitcast.13, s32[8]{0:T(128)} %shift_hbm.1), custom_call_target="tpu_custom_call" | custom-call | tf_op jit(solution)/shard_map/step/pallas_call | solution.py:361
  58.0 1.4 %put.1 = (bf16[32,16384]{1,0:T(8,128)(2,1)}, bf16[32,16384]{1,0:T(8,128)(2,1)}) custom-call(bf16[32,16384]{1,0:T(8,128)(2,1)S(1)} %get-tuple-element.6.refs_0_, bf16[32,16384]{1,0:T(8,128)(2,1)S(1)} %get-tuple-element.7.refs_1_), custom_call_target="tpu_custom_call" | custom-call | tf_op jit(solution)/shard_map/put/pallas_call | solution.py:335

commit v6 on v5

--- a/solution.py
+++ b/solution.py
@@ -246,10 +246,11 @@
     my_rows = pl.ds(pl.multiple_of(core * TILE[0], TILE[0]), TILE[0])
     my_lanes = pl.ds(pl.multiple_of(((y * count_x + x) * nx + gx) * TILE[1], TILE[1]), TILE[1])
 
-    corner = [(0, 0), (0, 1), (0, count_x - 1), (1, 0), (count_y - 1, 0)][:5]
+    corner = [(0, 0), (0, 1), (0, count_x - 1), (1, 0), (count_y - 1, 0)]
     corner = sorted(set(corner))
     planes = min(4, nx)
     early = len(corner) * planes * cores
+    portions = min(4, columns)
 
     def give_to(there_y, there_x, there_gx, there_core):
         target = device_at(there_y, there_x, there_gx, there_core)
@@ -280,6 +281,9 @@
         return 0
 
     def give(step, _):
+        size = jnp.where(core == 0, -(-early // columns), -(-early // portions))
+        start, stop = (jnp.minimum(n * size, early) for n in (step, step + 1))
+        lax.fori_loop(start, stop, give_early, 0)
         there_y, there_x = column_at(columns - 1 - step)
         near = functools.reduce(
             jnp.logical_or, [(there_y == cy) & (there_x == cx) for cy, cx in corner]
@@ -299,7 +303,6 @@
         return 0
 
     with jax.named_scope("s6_give"):
-        lax.fori_loop(0, early, give_early, 0)
         lax.fori_loop(0, columns, give, 0)
     mixed_ref[my_rows, my_lanes] = done[me]
 

time: 59.9 us -> 59.7 us (level)
  the two profiles are of different devices: /device:TPU:1 before, /device:TPU:16 now
where the time goes in v6:
time: 59.7 us; the launch traced here: 59.5 us
  Pallas kernels  58.9 us (99%)
  between operations  0.64 us (1%)
    pallas_call x1, Pallas kernels, shards(): pl.pallas_call(functools.partial(kernel, sizes), out_shape=[pltpu.VMEM((r...  57.5 us
    pallas_call x1, Pallas kernels, put(): pl.pallas_call(put_kernel, out_shape=[pltpu.HBM(a.shape, a.dtype) for a i...  1.38 us

profile of v6, /device:TPU:16, one launch (start us, length us, event | category | flops | bytes accessed | tf_op | source)
XLA Modules:
  0.0 59.5 jit_solution(9077798779272851506)
XLA Ops:
  0.6 57.5 %step.1 = (bf16[32,16384]{1,0:T(8,128)(2,1)S(1)}, bf16[32,16384]{1,0:T(8,128)(2,1)S(1)}) custom-call(bf16[32,256]{1,0:T(8,128)(2,1)} %bitcast.12, bf16[256,16384]{1,0:T(8,128)(2,1)} %bitcast.9, bf16[32,16384]{1,0:T(8,128)(2,1)} %bitcast.10, bf16[32,16384]{1,0:T(8,128)(2,1)} %bitcast.11, s32[1,256]{1,0:T(1,128)} %bitcast.13, s32[8]{0:T(128)} %shift_hbm.1), custom_call_target="tpu_custom_call" | custom-call | tf_op jit(solution)/shard_map/step/pallas_call | solution.py:364
  58.1 1.4 %put.1 = (bf16[32,16384]{1,0:T(8,128)(2,1)}, bf16[32,16384]{1,0:T(8,128)(2,1)}) custom-call(bf16[32,16384]{1,0:T(8,128)(2,1)S(1)} %get-tuple-element.6.refs_0_, bf16[32,16384]{1,0:T(8,128)(2,1)S(1)} %get-tuple-element.7.refs_1_), custom_call_target="tpu_custom_call" | custom-call | tf_op jit(solution)/shard_map/put/pallas_call | solution.py:338
